TPU v7x, 32 devices: a whole 2x2x4 slice. The times are simulated.
32 devices in a mesh: table: 16 (over z, y, x), dp: 2 (over core).
Axes of the slice: x: 2, y: 2, z: 4, core: 2. Of those that a mesh axis runs over, the one named last changes fastest.
Arguments:
- tables: bfloat16 [4, 65536, 128], P(None, 'table'), may hold values from -6 to 6
- owner_ids: int32 [32, 4, 256, 1], P(('table', 'dp')), may hold values from 0 to 15; in each aligned block of 256 rows (0 to 255, 256 to 511, ..., all dimensions but the last counted through in order) at most 32 rows name the same one
- row_ids: int32 [32, 4, 256], P(('table', 'dp')), may hold values from 0 to 4095
- session_of: int32 [32, 256], P(('table', 'dp')), may hold values from 0 to 1, never falling along the last dimension, each value on 1 to 200 neighbouring positions
- relevance: float32 [32, 256], P(('table', 'dp')), may hold values from 0.1 to 10
- logit_bias: float32 [32, 256], P(('table', 'dp')), may hold values from -400 to 400
- w_hidden: float32 [512, 512], replicated, may hold values from -0.25 to 0.25
- bias_hidden: float32 [512], replicated, may hold values from -3 to 3
- w_score: float32 [512], replicated, may hold values from -0.9 to 0.9
Outputs:
- emb_step: float32 [4, 65536, 128], P(None, ('table', 'dp'))
- step_hidden: float32 [512, 512], replicated
- step_bias: float32 [512], replicated
- step_score: float32 [512], replicated
- loss: float32 [], replicated
Inputs may be any that keep to these rules, and one draw needn't show every extreme that they name: `owner_ids`: among one device's impressions, for one table, at most 32 name the same owner. `session_of`: session numbers never fall along a device's impressions; each of a device's 2 sessions has 1 to 200 impressions.
All inputs are finite; a program needn't handle non-finite values.
Results may differ from a plain program's by a relative error of at most 0.001.
The roundings to bfloat16 on the way count: a program that leaves them out, or rounds other values in their place, can miss the bound.
Values may be sent and summed in bfloat16 or wider, within the bound.
A program may use at most 64 MiB of HBM per device.

v0:
```python
import jax
import jax.numpy as jnp
from jax import lax
from jax.sharding import PartitionSpec as P

SESS_DEV = 2


def silu_slope(pre_val):
    logistic = jax.nn.sigmoid(pre_val)
    return logistic * (1.0 + pre_val * (1.0 - logistic))


def session_terms(scores, session_ids, relevance, sessions):
    member = session_ids[None, :] == jnp.arange(sessions, dtype=jnp.int32)[:, None]
    highest = jnp.max(jnp.where(member, scores[None, :], -jnp.inf), axis=1)
    highest_each = jnp.sum(jnp.where(member, highest[:, None], 0.0), axis=0)
    shifted = scores - highest_each
    exponent = jnp.exp(shifted)
    totals = jnp.sum(jnp.where(member, exponent[None, :], 0.0), axis=1)
    weights = jnp.sum(jnp.where(member, relevance[None, :], 0.0), axis=1)
    total_each = jnp.sum(jnp.where(member, totals[:, None], 0.0), axis=0)
    weight_each = jnp.sum(jnp.where(member, weights[:, None], 0.0), axis=0)
    probability = exponent / total_each
    target = relevance / weight_each
    loss_sum = jnp.sum(jnp.log(totals)) - jnp.sum(target * shifted)
    return (loss_sum, probability - target)


def selector(indices, count):
    return (indices[:, None] == jnp.arange(count, dtype=jnp.int32)[None, :]).astype(jnp.bfloat16)


def pick_rows(indices, source):
    return jnp.dot(
        selector(indices, source.shape[0]), source, preferred_element_type=jnp.float32
    ).astype(jnp.bfloat16)


def place_rows(indices, values, count):
    return lax.dot_general(
        selector(indices, count),
        values,
        (((0,), (0,)), ((), ())),
        preferred_element_type=jnp.float32,
    )


def on_device(
    tables, owner_ids, row_ids, session_of, relevance, logit_bias, w_hidden, bias_hidden, w_score
):
    owners = lax.axis_size("table")
    devices = owners * lax.axis_size("dp")
    table_count, shard_rows, emb_width = tables.shape
    owner_now = owner_ids[0, :, :, 0]
    rows_now = row_ids[0]
    imp_count = owner_now.shape[1]
    capacity = 2 * imp_count // owners
    slot_total = owners * capacity
    one_hot = (owner_now[:, :, None] == jnp.arange(owners, dtype=jnp.int32)).astype(jnp.float32)
    places = jnp.arange(imp_count, dtype=jnp.int32)
    lower_tri = (places[:, None] >= places[None, :]).astype(jnp.float32)
    running = jnp.einsum("ij,tjo->tio", lower_tri, one_hot, precision=lax.Precision.HIGHEST)
    rank_in = (jnp.sum(running * one_hot, axis=2) - 1.0).astype(jnp.int32)
    slot_of = owner_now * capacity + rank_in
    slot_hot = (slot_of[:, :, None] == jnp.arange(slot_total, dtype=jnp.int32)).astype(jnp.int32)
    wanted = jnp.sum(slot_hot * rows_now[:, :, None], axis=1) + shard_rows * (
        1 - jnp.sum(slot_hot, axis=1)
    )
    requested = lax.all_to_all(
        wanted.reshape(table_count, owners, capacity),
        "table",
        split_axis=1,
        concat_axis=1,
        tiled=True,
    )
    served = lax.map(
        lambda pair: pick_rows(pair[0], pair[1]),
        (requested.reshape(table_count, slot_total), tables),
    )
    served = served.reshape(table_count, owners, capacity, emb_width)
    hidden_bf = w_hidden.astype(jnp.bfloat16)
    returned = lax.all_to_all(served, "table", split_axis=1, concat_axis=1, tiled=True).reshape(
        table_count, slot_total, emb_width
    )
    gathered = lax.map(lambda pair: pick_rows(pair[0], pair[1]), (slot_of, returned))
    inputs = jnp.transpose(gathered, (1, 0, 2)).reshape(imp_count, table_count * emb_width)
    pre_act = jnp.dot(inputs, hidden_bf, preferred_element_type=jnp.float32)
    pre_act = pre_act + bias_hidden
    hidden = jax.nn.silu(pre_act)
    scores = jnp.dot(hidden, w_score, precision=lax.Precision.HIGHEST) + logit_bias[0]
    loss_sum, score_grad = session_terms(scores, session_of[0], relevance[0], SESS_DEV)
    pre_grad = score_grad[:, None] * w_score[None, :] * silu_slope(pre_act)
    pre_grad_bf = pre_grad.astype(jnp.bfloat16)
    weight_grad = lax.dot_general(
        inputs, pre_grad_bf, (((0,), (0,)), ((), ())), preferred_element_type=jnp.float32
    )
    bias_grad = jnp.sum(pre_grad, axis=0)
    score_weight_grad = jnp.dot(score_grad, hidden, precision=lax.Precision.HIGHEST)
    input_grad = jnp.dot(pre_grad_bf, hidden_bf.T, preferred_element_type=jnp.float32).astype(
        jnp.bfloat16
    )
    input_grad = jnp.transpose(input_grad.reshape(imp_count, table_count, emb_width), (1, 0, 2))
    outgoing = lax.map(
        lambda pair: place_rows(pair[0], pair[1], slot_total).astype(jnp.bfloat16),
        (slot_of, input_grad),
    )
    incoming = lax.all_to_all(
        outgoing.reshape(table_count, owners, capacity, emb_width),
        "table",
        split_axis=1,
        concat_axis=1,
        tiled=True,
    )
    summed = lax.map(
        lambda pair: place_rows(pair[0], pair[1], shard_rows),
        (
            requested.reshape(table_count, slot_total),
            incoming.reshape(table_count, slot_total, emb_width),
        ),
    )
    own_rows = lax.psum_scatter(summed, "dp", scatter_dimension=1, tiled=True)
    emb_step = own_rows / (jnp.sqrt(jnp.mean(own_rows * own_rows, axis=2, keepdims=True)) + 1e-06)
    param_count = w_hidden.size + bias_hidden.size + w_score.size
    weight_tot, bias_tot, score_tot, loss_tot = lax.psum(
        (weight_grad, bias_grad, score_weight_grad, loss_sum), ("table", "dp")
    )
    mean_sq = (
        jnp.sum(weight_tot * weight_tot)
        + jnp.sum(bias_tot * bias_tot)
        + jnp.sum(score_tot * score_tot)
    ) / param_count
    factor = 1.0 / jnp.sqrt(mean_sq + 1e-06)
    step_hidden = weight_tot * factor
    loss = loss_tot / (SESS_DEV * devices)
    return (emb_step, step_hidden, bias_tot * factor, score_tot * factor, loss)


def solution(mesh):
    in_specs = (
        P(None, "table", None),
        P(("table", "dp"), None, None, None),
        P(("table", "dp"), None, None),
        P(("table", "dp"), None),
        P(("table", "dp"), None),
        P(("table", "dp"), None),
        P(),
        P(),
        P(),
    )
    out_specs = (P(None, ("table", "dp"), None), P(), P(), P(), P())
    return jax.shard_map(
        on_device, mesh=mesh, in_specs=in_specs, out_specs=out_specs, check_vma=False
    )
```

profile of v0, /device:TPU:0, one launch (start us, length us, event | category | flops | bytes accessed | tf_op | source)
XLA Modules:
  0.0 230.8 jit_solution(7807377824483772021)
XLA Ops:
  8.0 0.7 copy.45
  8.9 0.7 convert_add_fusion
  9.6 1.2 convert_reduce_fusion
  10.9 0.7 reshape.88
  11.6 8.3 %all-to-all-start = ((s32[16,1,128]{2,1,0:T(1,128)}), s32[16,1,128]{2,1,0:T(1,128)S(1)}, u32[]{:S(2)}, u32[]{:S(2)}) async-start(s32[16,1,128]{2,1,0:T(1,128)} %reshape.88), calls=%async_computation | async-start | bytes 16384 | tf_op jit(solution)/shard_map/all_to_all | solution.py:70
  20.0 7.2 %all-to-all-done = s32[16,1,128]{2,1,0:T(1,128)S(1)} async-done(((s32[16,1,128]{2,1,0:T(1,128)}), s32[16,1,128]{2,1,0:T(1,128)S(1)}, u32[]{:S(2)}, u32[]{:S(2)}) %all-to-all-start) | async-done | bytes 8224 | tf_op jit(solution)/shard_map/all_to_all | solution.py:70
  27.2 0.5 broadcast.55
  27.7 0.7 reduce
  28.7 11.4 %while.40 = (s32[]{:T(128)}, bf16[4,512,128]{2,1,0:T(8,128)(2,1)S(1)}, s32[4,512]{1,0:T(4,128)S(1)}, bf16[4,4096,128]{2,1,0:T(8,128)(2,1)}, s32[]{:T(128)}) while((s32[]{:T(128)}, bf16[4,512,128]{2,1,0:T(8,128)(2,1)S(1)}, s32[4,512]{1,0:T(4,128)S(1)}, bf16[4,4096,128]{2,1,0:T(8,128)(2,1)}, s32[]{:T(128)}) %tuple.66), condition=%wide.region_4.5_spmd, body=%wide.region_3.4_spmd.sunk | while | flops 539033600 | bytes 1186889 | solution.py:77
  28.7 2.8 %fusion.58 = bf16[4,512,128]{2,1,0:T(8,128)(2,1)S(1)} fusion(bf16[4,512,128]{2,1,0:T(8,128)(2,1)S(1)} %get-tuple-element.248, s32[]{:T(128)S(6)} %copy.55, s32[512]{0:T(512)S(1)} %bitcast.108, bf16[4,4096,128]{2,1,0:T(8,128)(2,1)} %get-tuple-element.255), kind=kOutput, calls=%fused_computation.5.clone.1 | convolution fusion | flops 539033600 | bytes 1182720 | tf_op jit(solution)/shard_map/while/body/eval_jaxpr/dot_general | solution.py:35
  31.5 2.8 %fusion.58 = bf16[4,512,128]{2,1,0:T(8,128)(2,1)S(1)} fusion(bf16[4,512,128]{2,1,0:T(8,128)(2,1)S(1)} %get-tuple-element.248, s32[]{:T(128)S(6)} %copy.55, s32[512]{0:T(512)S(1)} %bitcast.108, bf16[4,4096,128]{2,1,0:T(8,128)(2,1)} %get-tuple-element.255), kind=kOutput, calls=%fused_computation.5.clone.1 | convolution fusion | flops 539033600 | bytes 1182720 | tf_op jit(solution)/shard_map/while/body/eval_jaxpr/dot_general | solution.py:35
  34.4 2.8 %fusion.58 = bf16[4,512,128]{2,1,0:T(8,128)(2,1)S(1)} fusion(bf16[4,512,128]{2,1,0:T(8,128)(2,1)S(1)} %get-tuple-element.248, s32[]{:T(128)S(6)} %copy.55, s32[512]{0:T(512)S(1)} %bitcast.108, bf16[4,4096,128]{2,1,0:T(8,128)(2,1)} %get-tuple-element.255), kind=kOutput, calls=%fused_computation.5.clone.1 | convolution fusion | flops 539033600 | bytes 1182720 | tf_op jit(solution)/shard_map/while/body/eval_jaxpr/dot_general | solution.py:35
  37.2 2.8 %fusion.58 = bf16[4,512,128]{2,1,0:T(8,128)(2,1)S(1)} fusion(bf16[4,512,128]{2,1,0:T(8,128)(2,1)S(1)} %get-tuple-element.248, s32[]{:T(128)S(6)} %copy.55, s32[512]{0:T(512)S(1)} %bitcast.108, bf16[4,4096,128]{2,1,0:T(8,128)(2,1)} %get-tuple-element.255), kind=kOutput, calls=%fused_computation.5.clone.1 | convolution fusion | flops 539033600 | bytes 1182720 | tf_op jit(solution)/shard_map/while/body/eval_jaxpr/dot_general | solution.py:35
  40.1 0.9 copy.29
  40.9 3.6 %all-to-all-start.1 = ((bf16[4,16,32,128]{3,2,0,1:T(8,128)(2,1)}), bf16[4,16,32,128]{3,2,0,1:T(8,128)(2,1)S(1)}, u32[]{:S(2)}, u32[]{:S(2)}) async-start(bf16[4,16,32,128]{3,2,0,1:T(8,128)(2,1)} %copy.29), calls=%async_computation.1 | async-start | bytes 1048576 | tf_op jit(solution)/shard_map/all_to_all | solution.py:83
  44.5 13.9 %all-to-all-done.1 = bf16[4,16,32,128]{3,2,0,1:T(8,128)(2,1)S(1)} async-done(((bf16[4,16,32,128]{3,2,0,1:T(8,128)(2,1)}), bf16[4,16,32,128]{3,2,0,1:T(8,128)(2,1)S(1)}, u32[]{:S(2)}, u32[]{:S(2)}) %all-to-all-start.1) | async-done | bytes 524320 | tf_op jit(solution)/shard_map/all_to_all | solution.py:83
  58.5 1.8 while.41
  59.0 0.3 fusion.60
  59.9 0.3 fusion.60
  60.3 0.3 convolution_add_fusion
  60.7 0.6 fusion.39
  61.8 0.6 multiply_reduce_fusion.4
  62.4 0.4 fusion.26
  63.0 1.9 while.42
  63.0 0.4 fusion.62
  63.4 0.4 fusion.62
  63.9 0.4 fusion.62
  64.4 0.4 fusion.62
  64.8 0.9 copy.33
  65.7 3.8 %all-to-all-start.2 = ((bf16[4,16,32,128]{3,2,0,1:T(8,128)(2,1)}), bf16[4,16,32,128]{3,2,0,1:T(8,128)(2,1)S(1)}, u32[]{:S(2)}, u32[]{:S(2)}) async-start(bf16[4,16,32,128]{3,2,0,1:T(8,128)(2,1)} %copy.33), calls=%async_computation.2 | async-start | bytes 1048576 | tf_op jit(solution)/shard_map/all_to_all | solution.py:108
  69.5 1.4 fusion.34
  71.1 12.4 %all-to-all-done.2 = bf16[4,16,32,128]{3,2,0,1:T(8,128)(2,1)S(1)} async-done(((bf16[4,16,32,128]{3,2,0,1:T(8,128)(2,1)}), bf16[4,16,32,128]{3,2,0,1:T(8,128)(2,1)S(1)}, u32[]{:S(2)}, u32[]{:S(2)}) %all-to-all-start.2) | async-done | bytes 524320 | tf_op jit(solution)/shard_map/all_to_all | solution.py:108
  83.5 15.1 %while.43 = (s32[]{:T(128)}, f32[4,4096,128]{2,1,0:T(8,128)}, s32[4,512]{1,0:T(4,128)S(1)}, bf16[4,512,128]{2,1,0:T(8,128)(2,1)S(1)}, s32[]{:T(128)}) while((s32[]{:T(128)}, f32[4,4096,128]{2,1,0:T(8,128)}, s32[4,512]{1,0:T(4,128)S(1)}, bf16[4,512,128]{2,1,0:T(8,128)(2,1)S(1)}, s32[]{:T(128)}) %tuple.85), condition=%wide.region_16.17_spmd, body=%wide.region_15.16_spmd.sunk | while | flops 538968064 | bytes 2235465 | solution.py:115
  83.6 3.8 %fusion.64 = f32[4,4096,128]{2,1,0:T(8,128)} fusion(f32[4,4096,128]{2,1,0:T(8,128)} %get-tuple-element.293, s32[]{:T(128)S(6)} %copy.73, s32[512]{0:T(512)S(1)} %bitcast.109, bf16[4,512,128]{2,1,0:T(8,128)(2,1)S(1)} %get-tuple-element.300), kind=kOutput, calls=%fused_computation.31.clone.1 | convolution fusion | flops 538968064 | bytes 2231296 | tf_op jit(solution)/shard_map/while/body/eval_jaxpr/dot_general | solution.py:41
  87.4 3.7 %fusion.64 = f32[4,4096,128]{2,1,0:T(8,128)} fusion(f32[4,4096,128]{2,1,0:T(8,128)} %get-tuple-element.293, s32[]{:T(128)S(6)} %copy.73, s32[512]{0:T(512)S(1)} %bitcast.109, bf16[4,512,128]{2,1,0:T(8,128)(2,1)S(1)} %get-tuple-element.300), kind=kOutput, calls=%fused_computation.31.clone.1 | convolution fusion | flops 538968064 | bytes 2231296 | tf_op jit(solution)/shard_map/while/body/eval_jaxpr/dot_general | solution.py:41
  91.1 3.8 %fusion.64 = f32[4,4096,128]{2,1,0:T(8,128)} fusion(f32[4,4096,128]{2,1,0:T(8,128)} %get-tuple-element.293, s32[]{:T(128)S(6)} %copy.73, s32[512]{0:T(512)S(1)} %bitcast.109, bf16[4,512,128]{2,1,0:T(8,128)(2,1)S(1)} %get-tuple-element.300), kind=kOutput, calls=%fused_computation.31.clone.1 | convolution fusion | flops 538968064 | bytes 2231296 | tf_op jit(solution)/shard_map/while/body/eval_jaxpr/dot_general | solution.py:41
  94.9 3.8 %fusion.64 = f32[4,4096,128]{2,1,0:T(8,128)} fusion(f32[4,4096,128]{2,1,0:T(8,128)} %get-tuple-element.293, s32[]{:T(128)S(6)} %copy.73, s32[512]{0:T(512)S(1)} %bitcast.109, bf16[4,512,128]{2,1,0:T(8,128)(2,1)S(1)} %get-tuple-element.300), kind=kOutput, calls=%fused_computation.31.clone.1 | convolution fusion | flops 538968064 | bytes 2231296 | tf_op jit(solution)/shard_map/while/body/eval_jaxpr/dot_general | solution.py:41
  98.7 0.6 log_reduce_fusion
  100.8 0.5 fusion.37
  101.3 39.0 %all-reduce = (f32[512]{0:T(512)S(1)}, f32[512]{0:T(512)S(1)}, f32[]{:T(128)}) all-reduce(f32[512]{0:T(512)S(1)} %fusion.44, f32[512]{0:T(512)S(1)} %bitcast.122, f32[]{:T(128)S(6)} %sub.30), channel_id=1, replica_groups=mesh['table'=16,'dp'=2] {'table','dp'}, use_global_device_ids=true, to_apply=%region_22.23 | all-reduce | flops 1025 | bytes 8200 | tf_op jit(solution)/shard_map/psum | solution.py:125
  140.9 0.6 multiply_reduce_fusion.2
  141.6 66.5 %all-reduce.3.cloned.1.call-done = f32[512,512]{1,0:T(8,128)} async-done(((f32[512,512]{1,0:T(8,128)}), f32[512,512]{1,0:T(8,128)}) %all-reduce.3.cloned.1.call-update) | async-done | bytes 1048592 | tf_op jit(solution)/shard_map/psum | solution.py:125
  208.1 2.1 multiply_reduce_fusion.1
  212.2 0.6 broadcast_multiply_fusion.2
  212.7 0.6 broadcast_multiply_fusion.1
  213.3 2.3 broadcast_multiply_fusion
  215.6 3.5 %multiply_reduce_fusion = f32[4,2048]{1,0:T(4,128)S(1)} fusion(f32[4,2048,128]{2,1,0:T(8,128)} %reduce-scatter.2.cloned.1.call-done), kind=kLoop, calls=%fused_computation.37 | loop fusion | flops 2088960 | bytes 4227072 | tf_op jit(solution)/shard_map/reduce_sum | solution.py:123
  219.2 3.1 %broadcast_divide_fusion = f32[4,2048,128]{2,1,0:T(8,128)} fusion(f32[4,2048,128]{2,1,0:T(8,128)S(1)} %copy-done, f32[4,2048]{1,0:T(4,128)S(1)} %sqrt_add_fusion), kind=kLoop, calls=%fused_computation.38 | loop fusion | flops 1048576 | bytes 8421376 | tf_op jit(solution)/shard_map/div | solution.py:123
  (68 shorter events, 2.8 us)
Async XLA Ops:
  11.6 15.6 %all-to-all-start = ((s32[16,1,128]{2,1,0:T(1,128)}), s32[16,1,128]{2,1,0:T(1,128)S(1)}, u32[]{:S(2)}, u32[]{:S(2)}) async-start(s32[16,1,128]{2,1,0:T(1,128)} %reshape.88), calls=%async_computation | async-start | bytes 16384 | tf_op jit(solution)/shard_map/all_to_all | solution.py:70
  40.0 20.3 %copy-start.1 = (f32[512,512]{1,0:T(8,128)S(1)}, f32[512,512]{1,0:T(8,128)}, u32[]{:S(2)}) copy-start(f32[512,512]{1,0:T(8,128)} %param.23) | copy-start | bytes 3145732
  40.0 20.3 %copy-start.5 = (f32[512]{0:T(512)S(1)}, f32[512]{0:T(512)}, u32[]{:S(2)}) copy-start(f32[512]{0:T(512)} %param.24) | copy-start | bytes 6148
  40.0 20.6 %copy-start.4 = (f32[512]{0:T(512)S(1)}, f32[512]{0:T(512)}, u32[]{:S(2)}) copy-start(f32[512]{0:T(512)} %param.25) | copy-start | bytes 6148
  40.9 17.6 %all-to-all-start.1 = ((bf16[4,16,32,128]{3,2,0,1:T(8,128)(2,1)}), bf16[4,16,32,128]{3,2,0,1:T(8,128)(2,1)S(1)}, u32[]{:S(2)}, u32[]{:S(2)}) async-start(bf16[4,16,32,128]{3,2,0,1:T(8,128)(2,1)} %copy.29), calls=%async_computation.1 | async-start | bytes 1048576 | tf_op jit(solution)/shard_map/all_to_all | solution.py:83
  44.5 16.8 %copy-start.6 = (f32[1,256]{1,0:T(1,128)S(1)}, f32[1,256]{1,0:T(1,128)}, u32[]{:S(2)}) copy-start(f32[1,256]{1,0:T(1,128)} %param.22) | copy-start | bytes 3076
  44.5 16.8 %copy-start.2 = (s32[1,256]{1,0:T(1,128)S(1)}, s32[1,256]{1,0:T(1,128)}, u32[]{:S(2)}) copy-start(s32[1,256]{1,0:T(1,128)} %param.20) | copy-start | bytes 3076
  44.5 17.0 %copy-start.3 = (f32[1,256]{1,0:T(1,128)S(1)}, f32[1,256]{1,0:T(1,128)}, u32[]{:S(2)}) copy-start(f32[1,256]{1,0:T(1,128)} %param.21) | copy-start | bytes 3076
  65.7 17.8 %all-to-all-start.2 = ((bf16[4,16,32,128]{3,2,0,1:T(8,128)(2,1)}), bf16[4,16,32,128]{3,2,0,1:T(8,128)(2,1)S(1)}, u32[]{:S(2)}, u32[]{:S(2)}) async-start(bf16[4,16,32,128]{3,2,0,1:T(8,128)(2,1)} %copy.33), calls=%async_computation.2 | async-start | bytes 1048576 | tf_op jit(solution)/shard_map/all_to_all | solution.py:108
  69.5 138.6 %all-reduce.3.cloned.1.call-start = ((), (), s32[]{:S(2)}) async-start(), calls=%async_computation.5 | async-start | bytes 2097152 | tf_op jit(solution)/shard_map/psum | solution.py:125
  71.0 144.6 %reduce-scatter.2.cloned.1.call-start = ((), (), s32[]{:S(2)}) async-start(), calls=%async_computation.4 | async-start | bytes 12582912 | tf_op jit(solution)/shard_map/reduce_scatter | solution.py:122
  215.6 3.5 %copy-start = (f32[4,2048,128]{2,1,0:T(8,128)S(1)}, f32[4,2048,128]{2,1,0:T(8,128)}, u32[]{:S(2)}) copy-start(f32[4,2048,128]{2,1,0:T(8,128)} %reduce-scatter.2.cloned.1.call-done) | copy-start | bytes 12582916
Sparse Core Ops, SparseCore 0:
  76.1 131.9 all-reduce.2
Sparse Core Ops, SparseCore 1:
  98.8 14.4 reduce-scatter.1
where the time goes:
time: 232 us; the launch traced here: 231 us
  waiting for transfers between devices  100 us (43%)
  blocking collectives  39 us (17%)
  matrix products  32.6 us (14%)
  between operations  20.8 us (9%)
  other arithmetic  17.3 us (7%)
  starting transfers between devices  15.8 us (7%)
  local copies, waits for them, and re-layouts  4.78 us (2%)
    psum x1, waiting for transfers between devices, on_device(): lax.psum((weight_grad, bias_grad, score_weight_grad, loss_sum), ('table',...  66.5 us
    psum x1, blocking collectives, on_device(): lax.psum((weight_grad, bias_grad, score_weight_grad, loss_sum), ('table',...  39 us
    dot_general x8, matrix products, place_rows(): lax.dot_general(selector(indices, count), values, (((0,), (0,)), ((), ())...  16.8 us
    all_to_all x1, waiting for transfers between devices, on_device(): lax.all_to_all(served, 'table', split_axis=1, concat_axis=1, tiled=True)  13.9 us
    all_to_all x1, waiting for transfers between devices, on_device(): lax.all_to_all(outgoing.reshape(table_count, owners, capacity, emb_width)...  12.4 us
    dot_general x8, matrix products, pick_rows(): jnp.dot(selector(indices, source.shape[0]), source, preferred_element_typ...  12.4 us
    all_to_all x1, starting transfers between devices, on_device(): lax.all_to_all(wanted.reshape(table_count, owners, capacity), 'table', sp...  8.34 us
    all_to_all x1, waiting for transfers between devices, on_device(): lax.all_to_all(wanted.reshape(table_count, owners, capacity), 'table', sp...  7.23 us
  transfers between devices with their start and end apart: 5, of which 4 were waited for; matrix products, arithmetic and copies ran while one was open for 10% of the time, Pallas kernels for 0%

commit v1 on v0

--- a/solution.py
+++ b/solution.py
@@ -105,12 +105,17 @@
         lambda pair: place_rows(pair[0], pair[1], slot_total).astype(jnp.bfloat16),
         (slot_of, input_grad),
     )
-    incoming = lax.all_to_all(
-        outgoing.reshape(table_count, owners, capacity, emb_width),
-        "table",
-        split_axis=1,
-        concat_axis=1,
-        tiled=True,
+
+    def bands_define(inner_x, ax_name, d0, d_out):
+        return jnp.concatenate(
+            lax.all_to_all(
+                jnp.stack(jnp.split(inner_x, lax.axis_size(ax_name), d0)), ax_name, 0, 0
+            ),
+            d_out,
+        )
+
+    incoming = bands_define(
+        outgoing.reshape(table_count, owners, capacity, emb_width), "table", 1, 1
     )
     summed = lax.map(
         lambda pair: place_rows(pair[0], pair[1], shard_rows),

time: 232 us -> 241 us (1.039)
  local copies, waits for them, and re-layouts: 4.78 us -> 13.8 us
    unnamed x17 -> x32, local copies, waits for them, and re-layouts: 1.51 us -> 10.8 us
where the time goes in v1:
time: 241 us; the launch traced here: 240 us
  waiting for transfers between devices  100 us (41%)
  blocking collectives  39 us (16%)
  matrix products  32.6 us (14%)
  between operations  20.8 us (9%)
  other arithmetic  17.3 us (7%)
  starting transfers between devices  15.8 us (7%)
  local copies, waits for them, and re-layouts  13.8 us (6%)
    psum x1, waiting for transfers between devices, on_device(): lax.psum((weight_grad, bias_grad, score_weight_grad, loss_sum), ('table',...  66.5 us
    psum x1, blocking collectives, on_device(): lax.psum((weight_grad, bias_grad, score_weight_grad, loss_sum), ('table',...  39 us
    dot_general x8, matrix products, place_rows(): lax.dot_general(selector(indices, count), values, (((0,), (0,)), ((), ())...  16.8 us
    all_to_all x1, waiting for transfers between devices, on_device(): lax.all_to_all(served, 'table', split_axis=1, concat_axis=1, tiled=True)  13.9 us
    all_to_all x1, waiting for transfers between devices, bands_define(): lax.all_to_all(jnp.stack(jnp.split(inner_x, lax.axis_size(ax_name), d0)),...  12.4 us
    dot_general x8, matrix products, pick_rows(): jnp.dot(selector(indices, source.shape[0]), source, preferred_element_typ...  12.4 us
    unnamed x32, local copies, waits for them, and re-layouts  10.8 us
    all_to_all x1, starting transfers between devices, on_device(): lax.all_to_all(wanted.reshape(table_count, owners, capacity), 'table', sp...  8.34 us
  transfers between devices with their start and end apart: 5, of which 4 were waited for; matrix products, arithmetic and copies ran while one was open for 10% of the time, Pallas kernels for 0%

profile of v1, /device:TPU:0, one launch (start us, length us, event | category | flops | bytes accessed | tf_op | source)
XLA Modules:
  0.0 239.9 jit_solution(7184889849275414496)
XLA Ops:
  8.0 0.7 copy.120
  8.9 0.7 convert_add_fusion
  9.6 1.2 convert_reduce_fusion
  10.9 0.7 reshape.88
  11.6 8.3 %all-to-all-start = ((s32[16,1,128]{2,1,0:T(1,128)}), s32[16,1,128]{2,1,0:T(1,128)S(1)}, u32[]{:S(2)}, u32[]{:S(2)}) async-start(s32[16,1,128]{2,1,0:T(1,128)} %reshape.88), calls=%async_computation | async-start | bytes 16384 | tf_op jit(solution)/shard_map/all_to_all | solution.py:70
  20.0 7.2 %all-to-all-done = s32[16,1,128]{2,1,0:T(1,128)S(1)} async-done(((s32[16,1,128]{2,1,0:T(1,128)}), s32[16,1,128]{2,1,0:T(1,128)S(1)}, u32[]{:S(2)}, u32[]{:S(2)}) %all-to-all-start) | async-done | bytes 8224 | tf_op jit(solution)/shard_map/all_to_all | solution.py:70
  27.7 0.7 reduce
  28.6 11.4 %while.40 = (s32[]{:T(128)}, bf16[4,512,128]{2,1,0:T(8,128)(2,1)S(1)}, s32[4,512]{1,0:T(4,128)S(1)}, bf16[4,4096,128]{2,1,0:T(8,128)(2,1)}, s32[]{:T(128)}) while((s32[]{:T(128)}, bf16[4,512,128]{2,1,0:T(8,128)(2,1)S(1)}, s32[4,512]{1,0:T(4,128)S(1)}, bf16[4,4096,128]{2,1,0:T(8,128)(2,1)}, s32[]{:T(128)}) %tuple.66), condition=%wide.region_4.5_spmd, body=%wide.region_3.4_spmd.sunk | while | flops 539033600 | bytes 1186889 | solution.py:77
  28.7 2.8 %fusion.58 = bf16[4,512,128]{2,1,0:T(8,128)(2,1)S(1)} fusion(bf16[4,512,128]{2,1,0:T(8,128)(2,1)S(1)} %get-tuple-element.248, s32[]{:T(128)S(6)} %copy.130, s32[512]{0:T(512)S(1)} %bitcast.219, bf16[4,4096,128]{2,1,0:T(8,128)(2,1)} %get-tuple-element.255), kind=kOutput, calls=%fused_computation.5.clone.1 | convolution fusion | flops 539033600 | bytes 1182720 | tf_op jit(solution)/shard_map/while/body/eval_jaxpr/dot_general | solution.py:35
  31.5 2.8 %fusion.58 = bf16[4,512,128]{2,1,0:T(8,128)(2,1)S(1)} fusion(bf16[4,512,128]{2,1,0:T(8,128)(2,1)S(1)} %get-tuple-element.248, s32[]{:T(128)S(6)} %copy.130, s32[512]{0:T(512)S(1)} %bitcast.219, bf16[4,4096,128]{2,1,0:T(8,128)(2,1)} %get-tuple-element.255), kind=kOutput, calls=%fused_computation.5.clone.1 | convolution fusion | flops 539033600 | bytes 1182720 | tf_op jit(solution)/shard_map/while/body/eval_jaxpr/dot_general | solution.py:35
  34.4 2.8 %fusion.58 = bf16[4,512,128]{2,1,0:T(8,128)(2,1)S(1)} fusion(bf16[4,512,128]{2,1,0:T(8,128)(2,1)S(1)} %get-tuple-element.248, s32[]{:T(128)S(6)} %copy.130, s32[512]{0:T(512)S(1)} %bitcast.219, bf16[4,4096,128]{2,1,0:T(8,128)(2,1)} %get-tuple-element.255), kind=kOutput, calls=%fused_computation.5.clone.1 | convolution fusion | flops 539033600 | bytes 1182720 | tf_op jit(solution)/shard_map/while/body/eval_jaxpr/dot_general | solution.py:35
  37.2 2.8 %fusion.58 = bf16[4,512,128]{2,1,0:T(8,128)(2,1)S(1)} fusion(bf16[4,512,128]{2,1,0:T(8,128)(2,1)S(1)} %get-tuple-element.248, s32[]{:T(128)S(6)} %copy.130, s32[512]{0:T(512)S(1)} %bitcast.219, bf16[4,4096,128]{2,1,0:T(8,128)(2,1)} %get-tuple-element.255), kind=kOutput, calls=%fused_computation.5.clone.1 | convolution fusion | flops 539033600 | bytes 1182720 | tf_op jit(solution)/shard_map/while/body/eval_jaxpr/dot_general | solution.py:35
  40.1 0.9 copy.75
  40.9 3.6 %all-to-all-start.1 = ((bf16[4,16,32,128]{3,2,0,1:T(8,128)(2,1)}), bf16[4,16,32,128]{3,2,0,1:T(8,128)(2,1)S(1)}, u32[]{:S(2)}, u32[]{:S(2)}) async-start(bf16[4,16,32,128]{3,2,0,1:T(8,128)(2,1)} %copy.75), calls=%async_computation.1 | async-start | bytes 1048576 | tf_op jit(solution)/shard_map/all_to_all | solution.py:83
  44.5 13.9 %all-to-all-done.1 = bf16[4,16,32,128]{3,2,0,1:T(8,128)(2,1)S(1)} async-done(((bf16[4,16,32,128]{3,2,0,1:T(8,128)(2,1)}), bf16[4,16,32,128]{3,2,0,1:T(8,128)(2,1)S(1)}, u32[]{:S(2)}, u32[]{:S(2)}) %all-to-all-start.1) | async-done | bytes 524320 | tf_op jit(solution)/shard_map/all_to_all | solution.py:83
  58.5 1.8 while.41
  61.8 0.6 multiply_reduce_fusion.4
  62.9 1.9 while.42
  64.8 0.6 constant_dynamic-update-slice_fusion.16
  65.4 0.6 constant_dynamic-update-slice_fusion.15
  66.0 0.6 constant_dynamic-update-slice_fusion.14
  66.7 0.6 constant_dynamic-update-slice_fusion.13
  67.3 0.6 constant_dynamic-update-slice_fusion.12
  67.9 0.6 constant_dynamic-update-slice_fusion.11
  68.5 0.6 constant_dynamic-update-slice_fusion.10
  69.1 0.6 constant_dynamic-update-slice_fusion.9
  69.8 0.6 constant_dynamic-update-slice_fusion.8
  70.4 0.6 constant_dynamic-update-slice_fusion.7
  71.0 0.6 constant_dynamic-update-slice_fusion.6
  71.6 0.6 constant_dynamic-update-slice_fusion.5
  72.2 0.6 constant_dynamic-update-slice_fusion.4
  72.8 0.6 constant_dynamic-update-slice_fusion.3
  73.5 0.6 constant_dynamic-update-slice_fusion.2
  74.1 0.6 constant_dynamic-update-slice_fusion.1
  74.7 3.8 %all-to-all-start.2 = ((bf16[16,4,1,32,128]{4,3,1,2,0:T(8,128)(2,1)}), bf16[16,4,1,32,128]{4,3,1,2,0:T(8,128)(2,1)S(1)}, u32[]{:S(2)}, u32[]{:S(2)}) async-start(bf16[16,4,1,32,128]{4,3,1,2,0:T(8,128)(2,1)} %constant_dynamic-update-slice_fusion.1), calls=%async_computation.2 | async-start | bytes 1048576 | tf_op jit(solution)/shard_map/all_to_all | solution.py:111
  78.6 1.4 fusion.34
  80.1 12.4 %all-to-all-done.2 = bf16[16,4,1,32,128]{4,3,1,2,0:T(8,128)(2,1)S(1)} async-done(((bf16[16,4,1,32,128]{4,3,1,2,0:T(8,128)(2,1)}), bf16[16,4,1,32,128]{4,3,1,2,0:T(8,128)(2,1)S(1)}, u32[]{:S(2)}, u32[]{:S(2)}) %all-to-all-start.2) | async-done | bytes 524320 | tf_op jit(solution)/shard_map/all_to_all | solution.py:111
  92.6 15.1 %while.43 = (s32[]{:T(128)}, f32[4,4096,128]{2,1,0:T(8,128)}, s32[4,512]{1,0:T(4,128)S(1)}, bf16[4,512,128]{2,1,0:T(8,128)(2,1)S(1)}, s32[]{:T(128)}) while((s32[]{:T(128)}, f32[4,4096,128]{2,1,0:T(8,128)}, s32[4,512]{1,0:T(4,128)S(1)}, bf16[4,512,128]{2,1,0:T(8,128)(2,1)S(1)}, s32[]{:T(128)}) %tuple.85), condition=%wide.region_16.17_spmd, body=%wide.region_15.16_spmd.sunk | while | flops 538968064 | bytes 2235465 | solution.py:120
  92.6 3.8 %fusion.64 = f32[4,4096,128]{2,1,0:T(8,128)} fusion(f32[4,4096,128]{2,1,0:T(8,128)} %get-tuple-element.293, s32[]{:T(128)S(6)} %copy.163, s32[512]{0:T(512)S(1)} %bitcast.220, bf16[4,512,128]{2,1,0:T(8,128)(2,1)S(1)} %get-tuple-element.300), kind=kOutput, calls=%fused_computation.31.clone.1 | convolution fusion | flops 538968064 | bytes 2231296 | tf_op jit(solution)/shard_map/while/body/eval_jaxpr/dot_general | solution.py:41
  96.4 3.7 %fusion.64 = f32[4,4096,128]{2,1,0:T(8,128)} fusion(f32[4,4096,128]{2,1,0:T(8,128)} %get-tuple-element.293, s32[]{:T(128)S(6)} %copy.163, s32[512]{0:T(512)S(1)} %bitcast.220, bf16[4,512,128]{2,1,0:T(8,128)(2,1)S(1)} %get-tuple-element.300), kind=kOutput, calls=%fused_computation.31.clone.1 | convolution fusion | flops 538968064 | bytes 2231296 | tf_op jit(solution)/shard_map/while/body/eval_jaxpr/dot_general | solution.py:41
  100.1 3.8 %fusion.64 = f32[4,4096,128]{2,1,0:T(8,128)} fusion(f32[4,4096,128]{2,1,0:T(8,128)} %get-tuple-element.293, s32[]{:T(128)S(6)} %copy.163, s32[512]{0:T(512)S(1)} %bitcast.220, bf16[4,512,128]{2,1,0:T(8,128)(2,1)S(1)} %get-tuple-element.300), kind=kOutput, calls=%fused_computation.31.clone.1 | convolution fusion | flops 538968064 | bytes 2231296 | tf_op jit(solution)/shard_map/while/body/eval_jaxpr/dot_general | solution.py:41
  103.9 3.8 %fusion.64 = f32[4,4096,128]{2,1,0:T(8,128)} fusion(f32[4,4096,128]{2,1,0:T(8,128)} %get-tuple-element.293, s32[]{:T(128)S(6)} %copy.163, s32[512]{0:T(512)S(1)} %bitcast.220, bf16[4,512,128]{2,1,0:T(8,128)(2,1)S(1)} %get-tuple-element.300), kind=kOutput, calls=%fused_computation.31.clone.1 | convolution fusion | flops 538968064 | bytes 2231296 | tf_op jit(solution)/shard_map/while/body/eval_jaxpr/dot_general | solution.py:41
  110.3 39.0 %all-reduce = (f32[512]{0:T(512)S(1)}, f32[512]{0:T(512)S(1)}, f32[]{:T(128)}) all-reduce(f32[512]{0:T(512)S(1)} %fusion.44, f32[512]{0:T(512)S(1)} %bitcast.233, f32[]{:T(128)S(6)} %sub.30), channel_id=1, replica_groups=mesh['table'=16,'dp'=2] {'table','dp'}, use_global_device_ids=true, to_apply=%region_22.23 | all-reduce | flops 1025 | bytes 8200 | tf_op jit(solution)/shard_map/psum | solution.py:130
  150.6 66.5 %all-reduce.3.cloned.1.call-done = f32[512,512]{1,0:T(8,128)} async-done(((f32[512,512]{1,0:T(8,128)}), f32[512,512]{1,0:T(8,128)}) %all-reduce.3.cloned.1.call-update) | async-done | bytes 1048592 | tf_op jit(solution)/shard_map/psum | solution.py:130
  217.1 2.1 multiply_reduce_fusion.1
  222.4 2.3 broadcast_multiply_fusion
  224.6 3.5 %multiply_reduce_fusion = f32[4,2048]{1,0:T(4,128)S(1)} fusion(f32[4,2048,128]{2,1,0:T(8,128)} %reduce-scatter.2.cloned.1.call-done), kind=kLoop, calls=%fused_computation.37 | loop fusion | flops 2088960 | bytes 4227072 | tf_op jit(solution)/shard_map/reduce_sum | solution.py:128
  228.2 3.1 %broadcast_divide_fusion = f32[4,2048,128]{2,1,0:T(8,128)} fusion(f32[4,2048,128]{2,1,0:T(8,128)S(1)} %copy-done, f32[4,2048]{1,0:T(4,128)S(1)} %sqrt_add_fusion), kind=kLoop, calls=%fused_computation.38 | loop fusion | flops 1048576 | bytes 8421376 | tf_op jit(solution)/shard_map/div | solution.py:128
  (83 shorter events, 9.8 us)
Async XLA Ops:
  11.6 15.6 %all-to-all-start = ((s32[16,1,128]{2,1,0:T(1,128)}), s32[16,1,128]{2,1,0:T(1,128)S(1)}, u32[]{:S(2)}, u32[]{:S(2)}) async-start(s32[16,1,128]{2,1,0:T(1,128)} %reshape.88), calls=%async_computation | async-start | bytes 16384 | tf_op jit(solution)/shard_map/all_to_all | solution.py:70
  40.0 20.3 %copy-start.1 = (f32[512,512]{1,0:T(8,128)S(1)}, f32[512,512]{1,0:T(8,128)}, u32[]{:S(2)}) copy-start(f32[512,512]{1,0:T(8,128)} %param.23) | copy-start | bytes 3145732
  40.0 20.3 %copy-start.5 = (f32[512]{0:T(512)S(1)}, f32[512]{0:T(512)}, u32[]{:S(2)}) copy-start(f32[512]{0:T(512)} %param.24) | copy-start | bytes 6148
  40.0 20.6 %copy-start.4 = (f32[512]{0:T(512)S(1)}, f32[512]{0:T(512)}, u32[]{:S(2)}) copy-start(f32[512]{0:T(512)} %param.25) | copy-start | bytes 6148
  40.9 17.6 %all-to-all-start.1 = ((bf16[4,16,32,128]{3,2,0,1:T(8,128)(2,1)}), bf16[4,16,32,128]{3,2,0,1:T(8,128)(2,1)S(1)}, u32[]{:S(2)}, u32[]{:S(2)}) async-start(bf16[4,16,32,128]{3,2,0,1:T(8,128)(2,1)} %copy.75), calls=%async_computation.1 | async-start | bytes 1048576 | tf_op jit(solution)/shard_map/all_to_all | solution.py:83
  44.5 16.8 %copy-start.6 = (f32[1,256]{1,0:T(1,128)S(1)}, f32[1,256]{1,0:T(1,128)}, u32[]{:S(2)}) copy-start(f32[1,256]{1,0:T(1,128)} %param.22) | copy-start | bytes 3076
  44.5 16.8 %copy-start.2 = (s32[1,256]{1,0:T(1,128)S(1)}, s32[1,256]{1,0:T(1,128)}, u32[]{:S(2)}) copy-start(s32[1,256]{1,0:T(1,128)} %param.20) | copy-start | bytes 3076
  44.5 17.0 %copy-start.3 = (f32[1,256]{1,0:T(1,128)S(1)}, f32[1,256]{1,0:T(1,128)}, u32[]{:S(2)}) copy-start(f32[1,256]{1,0:T(1,128)} %param.21) | copy-start | bytes 3076
  74.7 17.8 %all-to-all-start.2 = ((bf16[16,4,1,32,128]{4,3,1,2,0:T(8,128)(2,1)}), bf16[16,4,1,32,128]{4,3,1,2,0:T(8,128)(2,1)S(1)}, u32[]{:S(2)}, u32[]{:S(2)}) async-start(bf16[16,4,1,32,128]{4,3,1,2,0:T(8,128)(2,1)} %constant_dynamic-update-slice_fusion.1), calls=%async_computation.2 | async-start | bytes 1048576 | tf_op jit(solution)/shard_map/all_to_all | solution.py:111
  78.5 138.6 %all-reduce.3.cloned.1.call-start = ((), (), s32[]{:S(2)}) async-start(), calls=%async_computation.5 | async-start | bytes 2097152 | tf_op jit(solution)/shard_map/psum | solution.py:130
  80.0 144.6 %reduce-scatter.2.cloned.1.call-start = ((), (), s32[]{:S(2)}) async-start(), calls=%async_computation.4 | async-start | bytes 12582912 | tf_op jit(solution)/shard_map/reduce_scatter | solution.py:127
  224.6 3.5 %copy-start = (f32[4,2048,128]{2,1,0:T(8,128)S(1)}, f32[4,2048,128]{2,1,0:T(8,128)}, u32[]{:S(2)}) copy-start(f32[4,2048,128]{2,1,0:T(8,128)} %reduce-scatter.2.cloned.1.call-done) | copy-start | bytes 12582916
Sparse Core Ops, SparseCore 0:
  85.1 131.9 all-reduce.2
Sparse Core Ops, SparseCore 1:
  107.8 14.4 reduce-scatter.1
